TPU v7x, 32 devices: a whole 2x2x4 slice. The times are simulated.
32 devices in a mesh: lon: 2 (over x), lat: 4 (over y, core), head: 4 (over z).
Axes of the slice: x: 2, y: 2, z: 4, core: 2. Of those that a mesh axis runs over, the one named last changes fastest.
Arguments:
- features: bfloat16 [8, 24, 24, 384], P(None, 'lat', 'lon'), may hold values from -6 to 6
- attend_weight: bfloat16 [3, 384, 384], P(None, None, 'head'), may hold values from -0.3125 to 0.3125
- output_weight: bfloat16 [384, 384], P('head'), may hold values from -0.3125 to 0.3125
- bias_table: float32 [64, 12, 3312], P(None, 'head'), may hold values from -3 to 304
- bias_type: int32 [4, 4], P(None, 'lat'), may hold values from 0 to 63
- window_shift: int32 [1], replicated, may hold values from 1 to 11
- grad_out: bfloat16 [8, 24, 24, 384], P(None, 'lat', 'lon'), may hold values from -6 to 6
Outputs:
- feature_grad: bfloat16 [8, 24, 24, 384], P(None, 'lat', 'lon', 'head')
- attend_grad: float32 [3, 384, 384], P(None, None, 'head')
- output_grad: float32 [384, 384], P('head')
- bias_grad: float32 [64, 12, 3312], P(None, 'head')
All inputs are finite; a program needn't handle non-finite values.
Results may differ from a plain program's by a relative error of at most 0.01.
Values may be sent and summed in bfloat16 or wider, within the bound.
A program may use at most 128 MiB of HBM per device.

v0:
```python
import functools

import jax
import jax.numpy as jnp
from jax import lax
from jax.experimental import pallas as pl
from jax.experimental.pallas import tpu as pltpu
from jax.sharding import PartitionSpec as P

WIN_LEVEL = 2
WIN_LAT = 6
WIN_LON = 12
ROWS = WIN_LEVEL * WIN_LAT
HALF = WIN_LON // 2
SPAN = 2 * WIN_LON - 1
PAD = 16
TOK = ROWS * PAD
F32 = jnp.float32
BF16 = jnp.bfloat16


def from_behind(x, axis, by):
    count = lax.axis_size(axis)
    return lax.ppermute(x, axis, [(i, (i + by) % count) for i in range(count)])


def dot(a, b, dims):
    return lax.dot_general(a, b, (dims, ((), ())), preferred_element_type=F32)


NN = ((1,), (0,))
NT = ((1,), (1,))
TN = ((0,), (0,))


def use_neighbour(shift, col):
    first = jnp.where(shift <= HALF, 0, shift)
    return (col >= first) & (col < jnp.where(shift <= HALF, shift, WIN_LON))


def block_kernel(heads, shift_ref, type_ref, x_ref, g_ref, low_ref, high_ref, aw_ref, ow_ref, table_ref,
                 piece_ref, grad_aw_ref, grad_ow_ref, grad_bias_ref,
                 xs, gs, proj, gproj, att, bias_a, bias_b, rel, table, sems):
    shift = shift_ref[0]
    wins = table.shape[0]
    width = x_ref.shape[-1]
    inner = aw_ref.shape[2]
    size = inner // heads
    part = WIN_LAT * SPAN
    copies = [
        pltpu.make_async_copy(table_ref.at[type_ref[w, 0]], table.at[w], sems.at[w]) for w in range(wins)
    ]
    for copy in copies:
        copy.start()

    lines = wins * ROWS
    col = lax.broadcasted_iota(jnp.int32, (lines, WIN_LON, width), 1)
    taken = use_neighbour(shift, col)
    for src, dst, n in ((x_ref, xs, 0), (g_ref, gs, 1)):
        near = jnp.concatenate([low_ref[n].astype(F32), high_ref[n].astype(F32)], axis=1)
        picked = jnp.where(taken, near, src[...].astype(F32))
        full = jnp.concatenate([picked, jnp.zeros((lines, PAD - WIN_LON, width), F32)], axis=1)
        dst[...] = full.astype(BF16).reshape(lines * PAD, width)
    tokens = xs[...]
    grads = gs[...]
    for c in range(3):
        proj[c] = dot(tokens, aw_ref[c], NN).astype(BF16)
    proj[3] = dot(grads, ow_ref[...], NT).astype(BF16)

    for copy in copies:
        copy.wait()
    rel[...] = jnp.zeros_like(rel)
    for w in range(wins):
        for k in range(WIN_LEVEL * WIN_LEVEL * WIN_LAT):
            zi, zj, ai = k // (WIN_LEVEL * WIN_LAT), k // WIN_LAT % WIN_LEVEL, k % WIN_LAT
            rel[zi * WIN_LAT + ai, w * heads:(w + 1) * heads, zj * part:(zj + 1) * part] = table[
                w, :, k * part:(k + 1) * part
            ]
    lanes = rel.shape[2]
    row = lax.broadcasted_iota(jnp.int32, (lanes, TOK), 0)
    key = lax.broadcasted_iota(jnp.int32, (lanes, TOK), 1)
    slot = key % PAD
    pos = slot + WIN_LON - shift
    pos = jnp.where(pos >= WIN_LON, pos - WIN_LON, pos)
    hit = (row == key // PAD * SPAN + WIN_LON - 1 - pos) & (slot < WIN_LON)
    spread = jnp.where(hit, 1.0, 0.0).astype(BF16)
    unused = jnp.where(lax.broadcasted_iota(jnp.int32, (1, TOK), 1) % PAD < WIN_LON, 0.0, -1e30)
    group = PAD
    flat = rel[...].reshape(ROWS * group, lanes)
    for c in range(PAD):
        if c < WIN_LON:
            place = lax.rem(c + WIN_LON - shift, WIN_LON)
            moved = pltpu.roll(flat, lanes - place, 1)
            one = moved.astype(BF16)
            rest = moved - one.astype(F32)
            two = rest.astype(BF16)
            three = (rest - two.astype(F32)).astype(BF16)
            out = dot(one, spread, NN) + dot(two, spread, NN) + dot(three, spread, NN) + unused
        else:
            out = jnp.zeros((ROWS * group, TOK), F32)
        for p in range(ROWS):
            base = (p * PAD + c) * group
            bias_a[base:base + group, :] = out[p * group:(p + 1) * group, :128]
            bias_b[base:base + group, :TOK - 128] = out[p * group:(p + 1) * group, 128:]

    scaling = size ** -0.5
    lane = lax.broadcasted_iota(jnp.int32, (TOK, inner), 1) // size
    for w in range(wins):
        span = slice(w * TOK, (w + 1) * TOK)
        q, k, v, ga = proj[0, span], proj[1, span], proj[2, span], proj[3, span]
        sums = [None] * 4
        for h in range(heads):
            e = w * heads + h
            mine = (lane == h).astype(BF16)
            qh, kh, vh, gah = q * mine, k * mine, v * mine, ga * mine
            rows = pl.ds(e, TOK, stride=group)
            bias = jnp.concatenate([bias_a[rows, :], bias_b[rows, :][:, :TOK - 128]], axis=1)
            scores = dot(qh, k, NT) * scaling + bias
            top = jnp.max(scores, axis=1, keepdims=True)
            raised = jnp.exp(scores - top)
            soft = raised * (1.0 / jnp.sum(raised, axis=1, keepdims=True))
            half = soft.astype(BF16)
            grad_soft = dot(gah, v, NT)
            both = soft * grad_soft
            grad_scores = both - soft * jnp.sum(both, axis=1, keepdims=True)
            bias_a[rows, :] = grad_scores[:, :128]
            bias_b[rows, :] = jnp.concatenate(
                [grad_scores[:, 128:], jnp.zeros((TOK, 256 - TOK), F32)], axis=1
            )
            gsh = grad_scores.astype(BF16)
            terms = (dot(half, vh, NN), dot(gsh, kh, NN), dot(gsh, qh, TN), dot(half, gah, TN))
            sums = [t if s is None else s + t for s, t in zip(sums, terms)]
        att[span] = sums[0].astype(BF16)
        gproj[0, span] = (sums[1] * scaling).astype(BF16)
        gproj[1, span] = (sums[2] * scaling).astype(BF16)
        gproj[2, span] = sums[3].astype(BF16)

    chunks, chunk = piece_ref.shape[0], piece_ref.shape[-1]
    for n in range(chunks):
        cols = slice(n * chunk, (n + 1) * chunk)
        total = sum(dot(gproj[c], aw_ref[c, cols, :], NT) for c in range(3))
        piece_ref[n] = total.reshape(lines, PAD, chunk)[:, :WIN_LON].astype(BF16)
    for c in range(3):
        grad_aw_ref[c] = dot(tokens, gproj[c], TN)
    grad_ow_ref[...] = dot(att[...], grads, TN)

    folded = jnp.zeros((ROWS * group, lanes), F32)
    for c in range(WIN_LON):
        place = lax.rem(c + WIN_LON - shift, WIN_LON)
        parts = []
        for p in range(ROWS):
            base = (p * PAD + c) * group
            parts.append(
                jnp.concatenate(
                    [bias_a[base:base + group, :], bias_b[base:base + group, :][:, :TOK - 128]], axis=1
                )
            )
        got = jnp.concatenate(parts, axis=0)
        one = got.astype(BF16)
        two = (got - one.astype(F32)).astype(BF16)
        folded = folded + pltpu.roll(dot(one, spread, NT) + dot(two, spread, NT), place, 1)
    rel[...] = folded.reshape(ROWS, group, lanes)
    for w in range(wins):
        for k in range(WIN_LEVEL * WIN_LEVEL * WIN_LAT):
            zi, zj, ai = k // (WIN_LEVEL * WIN_LAT), k // WIN_LAT % WIN_LEVEL, k % WIN_LAT
            grad_bias_ref[w, :, k * part:(k + 1) * part] = rel[
                zi * WIN_LAT + ai, w * heads:(w + 1) * heads, zj * part:(zj + 1) * part
            ]


def block_backward(features, grad_out, low, high, attend_weight, output_weight, bias_table, bias_type, shift):
    levels, lat_rows, lon_cols, width = features.shape
    heads, rel_total = bias_table.shape[1:]
    inner = attend_weight.shape[2]
    wins = levels // WIN_LEVEL
    lines = wins * ROWS
    chunks = lax.axis_size("head")
    vmem = pl.BlockSpec(memory_space=pltpu.VMEM)
    smem = pl.BlockSpec(memory_space=pltpu.SMEM)
    lanes = -(-ROWS * SPAN // 128) * 128
    total = lines * PAD
    return pl.pallas_call(
        functools.partial(block_kernel, heads),
        out_shape=(
            jax.ShapeDtypeStruct((chunks, lines, WIN_LON, width // chunks), BF16),
            jax.ShapeDtypeStruct(attend_weight.shape, F32),
            jax.ShapeDtypeStruct(output_weight.shape, F32),
            jax.ShapeDtypeStruct((wins, heads, rel_total), F32),
        ),
        in_specs=[smem, smem, vmem, vmem, vmem, vmem, vmem, vmem, pl.BlockSpec(memory_space=pl.ANY)],
        out_specs=(vmem, vmem, vmem, vmem),
        scratch_shapes=[
            pltpu.VMEM((total, width), BF16),
            pltpu.VMEM((total, width), BF16),
            pltpu.VMEM((4, total, inner), BF16),
            pltpu.VMEM((3, total, inner), BF16),
            pltpu.VMEM((total, inner), BF16),
            pltpu.VMEM((TOK * PAD, 128), F32),
            pltpu.VMEM((TOK * PAD, 128), F32),
            pltpu.VMEM((ROWS, PAD, lanes), F32),
            pltpu.VMEM((wins, heads, rel_total), F32),
            pltpu.SemaphoreType.DMA((wins,)),
        ],
        compiler_params=pltpu.CompilerParams(vmem_limit_bytes=50 * 1024 * 1024),
        cost_estimate=pl.CostEstimate(flops=10**9, bytes_accessed=10**7, transcendentals=10**6),
    )(
        shift,
        bias_type,
        features.reshape(lines, lon_cols, width),
        grad_out.reshape(lines, lon_cols, width),
        low,
        high,
        attend_weight,
        output_weight,
        bias_table,
    )


def swap_columns(low, high, shift):
    if lax.axis_size("lon") <= 2:
        got = from_behind(jnp.where(shift <= HALF, low, high), "lon", 1)
        return got, got
    return from_behind(low, "lon", -1), from_behind(high, "lon", 1)


def per_device(features, attend_weight, output_weight, bias_table, bias_type, window_shift, grad_out):
    shift = window_shift[0]
    levels, lat_rows, lon_cols, width = features.shape
    stacked = jnp.stack((features, grad_out)).reshape(2, levels * lat_rows, lon_cols, width)
    low, high = swap_columns(stacked[:, :, :HALF], stacked[:, :, HALF:], shift)
    pieces, grad_attend, grad_output, grad_bias = block_backward(
        features, grad_out, low, high, attend_weight, output_weight, bias_table, bias_type, window_shift
    )
    summed = lax.psum_scatter(pieces, "head", scatter_dimension=0, tiled=False)
    low, high = swap_columns(summed[:, :HALF], summed[:, HALF:], shift)
    taken = use_neighbour(shift, jnp.arange(lon_cols))[None, :, None]
    feature_grad = jnp.where(taken, jnp.concatenate((low, high), axis=1), summed)
    feature_grad = feature_grad.reshape(levels, lat_rows, lon_cols, -1)
    attend_grad, output_grad = lax.psum((grad_attend, grad_output), ("lon", "lat"))
    parts = lax.all_gather(grad_bias, ("lon", "lat")).reshape(-1, *bias_table.shape[1:])
    types = lax.all_gather(bias_type[:, 0], ("lon", "lat")).reshape(-1)
    selector = (types[:, None] == jnp.arange(bias_table.shape[0], dtype=jnp.int32)[None, :]).astype(F32)
    bias_grad = jnp.einsum("at,ahr->thr", selector, parts, precision=lax.Precision.HIGHEST)
    return (feature_grad, attend_grad, output_grad, bias_grad)


def solution(mesh):
    placed = (
        P(None, "lat", "lon", None),
        P(None, None, "head"),
        P("head", None),
        P(None, "head", None),
        P(None, "lat"),
        P(),
        P(None, "lat", "lon", None),
    )
    return jax.shard_map(
        per_device,
        mesh=mesh,
        in_specs=placed,
        out_specs=(
            P(None, "lat", "lon", "head"),
            P(None, None, "head"),
            P("head", None),
            P(None, "head", None),
        ),
        check_vma=False,
    )
```

profile of v0, /device:TPU:0, one launch (start us, length us, event | category | flops | bytes accessed | tf_op | source)
XLA Modules:
  0.0 140.0 jit_solution(10134770405133214256)
XLA Ops:
  8.0 0.0 copy-start.3
  8.0 0.0 reduce-scatter.2.cloned.1.call-start
  8.7 1.2 copy.39
  9.9 0.1 stack.9
  10.1 0.0 copy-done.3
  10.1 0.2 copy.40
  10.3 0.0 copy-start.2
  10.3 0.1 stack.10
  10.5 0.1 constant_dynamic-update-slice_fusion
  10.6 0.0 copy-start.1
  10.6 0.1 slice_select_fusion
  10.6 3.0 %collective-permute-start = (bf16[2,48,6,384]{3,1,2,0:T(8,128)(2,1)S(1)}, bf16[2,48,6,384]{3,1,2,0:T(8,128)(2,1)S(1)}, u32[]{:S(2)}, u32[]{:S(2)}) collective-permute-start(bf16[2,48,6,384]{3,1,2,0:T(8,128)(2,1)S(1)} %slice_select_fusion), channel_id=1, source_target_pairs={{0,16},{16,0},{1,17},{17,1},{2,18},{18,2},{3,19},{19,3},{4,20},{20... | collective-permute-start | bytes 1327112 | tf_op jit(solution)/shard_map/ppermute | solution.py:24
  13.7 0.0 copy-done.2
  13.7 0.1 copy.37
  13.8 0.1 copy.38
  13.8 0.0 copy-done.1
  13.9 0.0 copy-start.4
  13.9 0.0 copy-start.6
  13.9 0.0 copy-start
  13.9 3.5 %copy.45.table_ref = f32[64,3,3312]{2,1,0:T(4,128)} copy(f32[64,3,3312]{2,0,1:T(8,128)S(1)} %copy-done.1) | data formatting | bytes 5087232 | tf_op args[3]
  17.4 0.0 copy-done.4
  17.4 0.2 copy.44.aw_ref
  17.6 0.0 copy-done.6
  17.6 0.1 copy.41.type_ref
  17.7 6.2 %collective-permute-done = bf16[2,48,6,384]{3,1,2,0:T(8,128)(2,1)S(1)} collective-permute-done((bf16[2,48,6,384]{3,1,2,0:T(8,128)(2,1)S(1)}, bf16[2,48,6,384]{3,1,2,0:T(8,128)(2,1)S(1)}, u32[]{:S(2)}, u32[]{:S(2)}) %collective-permute-start) | collective-permute-done | bytes 442400 | tf_op jit(solution)/shard_map/ppermute | solution.py:24
  23.8 0.1 copy.42.low_ref.high_ref
  24.0 0.0 copy-done
  24.0 15.0 %shard_map.102 = (bf16[4,48,12,96]{3,2,1,0:T(8,128)(2,1)}, f32[3,384,96]{2,1,0:T(8,128)}, f32[96,384]{1,0:T(8,128)}, f32[4,3,3312]{2,1,0:T(4,128)}) custom-call(s32[1]{0:T(128)} %copy.58.shift_ref, s32[4,1]{1,0:T(4,128)S(1)} %copy.41.type_ref, bf16[48,12,384]{2,1,0:T(8,128)(2,1)S(1)} %bitcast.19, bf16[48,12,384]{2,1,0:T(8,128)(2,1)S(1)} %bitcast.20, ...), custom_call_target="tpu_custom_call" | custom-call | flops 1000000000 | bytes 10000000 | tf_op jit(solution)/shard_map/pallas_call | solution.py:182
  39.0 0.0 copy-start.7
  39.0 0.0 reduce-scatter.2.cloned.1.call-update
  39.0 0.0 all-reduce.4.cloned.1.call-start
  39.1 0.5 all-reduce.4.cloned.1.call-update
  39.6 0.0 all-gather.4.cloned.1.call-start
  39.7 0.5 all-gather.4.cloned.1.call-update
  40.2 0.0 copy-done.7
  40.2 0.6 dynamic-slice
  41.5 0.1 bitcast_dynamic-update-slice_fusion
  41.6 22.3 %reduce-scatter.2.cloned.1.call-done = bf16[1,48,12,96]{3,2,1,0:T(8,128)(2,1)} async-done(((bf16[4,48,12,96]{3,2,1,0:T(8,128)(2,1)}), bf16[1,48,12,96]{3,2,1,0:T(8,128)(2,1)}) %reduce-scatter.2.cloned.1.call-update) | async-done | bytes 110608 | tf_op jit(solution)/shard_map/reduce_scatter | solution.py:234
  63.8 1.0 slice_select_fusion.1
  64.9 1.6 %collective-permute-start.1 = (bf16[48,6,96]{2,1,0:T(8,128)(2,1)S(1)}, bf16[48,6,96]{2,1,0:T(8,128)(2,1)S(1)}, u32[]{:S(2)}, u32[]{:S(2)}) collective-permute-start(bf16[48,6,96]{2,1,0:T(8,128)(2,1)S(1)} %slice_select_fusion.1), channel_id=1, source_target_pairs={{0,16},{16,0},{1,17},{17,1},{2,18},{18,2},{3,19},{19,3},{4,20},{20... | collective-permute-start | bytes 165896 | tf_op jit(solution)/shard_map/ppermute | solution.py:24
  66.4 7.0 %all-reduce = s32[32]{0:T(128)S(1)} all-reduce(s32[32]{0:T(128)S(1)} %bitcast_dynamic-update-slice_fusion), channel_id=2, replica_groups=mesh['lon'=2,'lat'=4,'head'=4] {'lon','lat'}, use_global_device_ids=true, to_apply=%add | all-reduce | flops 32 | bytes 256
  73.5 26.2 %all-reduce.4.cloned.1.call-done = (f32[3,384,96]{2,1,0:T(8,128)}, f32[96,384]{1,0:T(8,128)}) async-done(((f32[3,384,96]{2,1,0:T(8,128)}, f32[96,384]{1,0:T(8,128)}), (f32[3,384,96]{2,1,0:T(8,128)}, f32[96,384]{1,0:T(8,128)})) %all-reduce.4.cloned.1.call-update) | async-done | bytes 589840 | tf_op jit(solution)/shard_map/psum | solution.py:239
  99.7 2.1 %copy.50 = f32[3,384,96]{1,2,0:T(8,128)} copy(f32[3,384,96]{2,1,0:T(8,128)} %get-tuple-element.24) | data formatting | bytes 884736
  101.7 0.0 collective-permute-done.1
  101.8 1.7 %maximum_select_fusion = bf16[8,6,12,96]{3,0,2,1:T(8,128)(2,1)} fusion(bf16[8,6,6,96]{3,0,2,1:T(8,128)(2,1)S(1)} %copy.46, bf16[8,6,12,96]{3,2,1,0:T(8,128)(2,1)} %bitcast.22, pred[12]{0:T(512)(128)(4,1)S(1)} %compare_and_fusion), kind=kLoop, calls=%fused_computation.3 | loop fusion | flops 110592 | bytes 276492 | tf_op jit(solution)/shard_map/jit(_where)/select_n | solution.py:237
  103.4 24.2 %all-gather.4.cloned.1.call-done = f32[32,3,3312]{2,1,0:T(4,128)} async-done(((f32[4,3,3312]{2,1,0:T(4,128)}), f32[32,3,3312]{2,1,0:T(4,128)}) %all-gather.4.cloned.1.call-update) | async-done | bytes 1271824 | tf_op jit(solution)/shard_map/all_gather | solution.py:240
  127.7 4.2 %fusion = f32[64,3,3312]{2,0,1:T(8,128)} fusion(f32[32,3,3312]{2,1,0:T(4,128)} %all-gather.4.cloned.1.call-done, s32[32]{0:T(128)S(1)} %all-reduce), kind=kOutput, calls=%fused_computation | convolution fusion | flops 244189184 | bytes 3815552 | tf_op jit(solution)/shard_map/at,ahr->thr/dot_general | solution.py:243
  131.9 0.7 copy.59
  (6 shorter events, 0.1 us)
Async XLA Ops:
  8.0 2.1 %copy-start.3 = (bf16[8,6,12,384]{3,0,2,1:T(8,128)(2,1)S(1)}, bf16[8,6,12,384]{3,0,2,1:T(8,128)(2,1)}, u32[]{:S(2)}) copy-start(bf16[8,6,12,384]{3,0,2,1:T(8,128)(2,1)} %param.13) | copy-start | bytes 1327108
  8.0 55.8 %reduce-scatter.2.cloned.1.call-start = ((), (), s32[]{:S(2)}) async-start(), calls=%async_computation.1 | async-start | bytes 983040 | tf_op jit(solution)/shard_map/reduce_scatter | solution.py:234
  10.3 3.4 %copy-start.2 = (bf16[8,6,12,384]{3,0,2,1:T(8,128)(2,1)S(1)}, bf16[8,6,12,384]{3,0,2,1:T(8,128)(2,1)}, u32[]{:S(2)}) copy-start(bf16[8,6,12,384]{3,0,2,1:T(8,128)(2,1)} %param.7) | copy-start | bytes 1327108
  10.6 3.3 %copy-start.1 = (f32[64,3,3312]{2,0,1:T(8,128)S(1)}, f32[64,3,3312]{2,0,1:T(8,128)}, u32[]{:S(2)}) copy-start(f32[64,3,3312]{2,0,1:T(8,128)} %param.10) | copy-start | bytes 7630852
  10.6 13.2 %collective-permute-start = (bf16[2,48,6,384]{3,1,2,0:T(8,128)(2,1)S(1)}, bf16[2,48,6,384]{3,1,2,0:T(8,128)(2,1)S(1)}, u32[]{:S(2)}, u32[]{:S(2)}) collective-permute-start(bf16[2,48,6,384]{3,1,2,0:T(8,128)(2,1)S(1)} %slice_select_fusion), channel_id=1, source_target_pairs={{0,16},{16,0},{1,17},{17,1},{2,18},{18,2},{3,19},{19,3},{4,20},{20... | collective-permute-start | bytes 1327112 | tf_op jit(solution)/shard_map/ppermute | solution.py:24
  13.9 3.5 %copy-start.4 = (bf16[3,384,96]{1,2,0:T(8,128)(2,1)S(1)}, bf16[3,384,96]{1,2,0:T(8,128)(2,1)}, u32[]{:S(2)}) copy-start(bf16[3,384,96]{1,2,0:T(8,128)(2,1)} %param.8) | copy-start | bytes 663556
  13.9 3.7 %copy-start.6 = (s32[4,1]{0,1:T(1,128)S(1)}, s32[4,1]{0,1:T(1,128)}, u32[]{:S(2)}) copy-start(s32[4,1]{0,1:T(1,128)} %param.11) | copy-start | bytes 52
  13.9 10.1 %copy-start = (bf16[96,384]{1,0:T(8,128)(2,1)S(1)}, bf16[96,384]{1,0:T(8,128)(2,1)}, u32[]{:S(2)}) copy-start(bf16[96,384]{1,0:T(8,128)(2,1)} %ow_ref.1) | copy-start | bytes 221188
  39.0 1.2 copy-start.7
  39.0 60.6 %all-reduce.4.cloned.1.call-start = ((), (), s32[]{:S(2)}) async-start(), calls=%async_computation.3 | async-start | bytes 1474560 | tf_op jit(solution)/shard_map/psum | solution.py:239
  39.6 88.1 %all-gather.4.cloned.1.call-start = ((), (), s32[]{:S(2)}) async-start(), calls=%async_computation.2 | async-start | bytes 1916928 | tf_op jit(solution)/shard_map/all_gather | solution.py:240
  64.9 36.9 %collective-permute-start.1 = (bf16[48,6,96]{2,1,0:T(8,128)(2,1)S(1)}, bf16[48,6,96]{2,1,0:T(8,128)(2,1)S(1)}, u32[]{:S(2)}, u32[]{:S(2)}) collective-permute-start(bf16[48,6,96]{2,1,0:T(8,128)(2,1)S(1)} %slice_select_fusion.1), channel_id=1, source_target_pairs={{0,16},{16,0},{1,17},{17,1},{2,18},{18,2},{3,19},{19,3},{4,20},{20... | collective-permute-start | bytes 165896 | tf_op jit(solution)/shard_map/ppermute | solution.py:24
  103.4 28.5 %copy-start.5 = (f32[96,384]{1,0:T(8,128)S(1)}, f32[96,384]{1,0:T(8,128)}, u32[]{:S(2)}) copy-start(f32[96,384]{1,0:T(8,128)} %get-tuple-element.28) | copy-start | bytes 442372
Sparse Core Ops, SparseCore 0:
  39.2 24.6 reduce-scatter.1
Sparse Core Ops, SparseCore 1:
  43.4 56.3 all-reduce.3
  101.4 26.2 all-gather.3
where the time goes:
time: 140 us
  waiting for transfers between devices  80 us (57%)
  between operations  17 us (12%)
  Pallas kernels  15 us (11%)
  local copies, waits for them, and re-layouts  9.26 us (7%)
  blocking collectives  7.01 us (5%)
  starting transfers between devices  4.71 us (3%)
  matrix products  4.21 us (3%)
  other arithmetic  2.77 us (2%)
    psum x1, waiting for transfers between devices, per_device(): lax.psum((grad_attend, grad_output), ('lon', 'lat'))  26.2 us
    all_gather x1, waiting for transfers between devices, per_device(): lax.all_gather(grad_bias, ('lon', 'lat')).reshape(-1, *bias_table.shape[1:])  24.2 us
    reduce_scatter x1, waiting for transfers between devices, per_device(): summed = lax.psum_scatter(pieces, 'head', scatter_dimension=0, tiled=False)  22.3 us
    pallas_call x1, Pallas kernels, block_backward(): pl.pallas_call(functools.partial(block_kernel, heads), out_shape=(jax.Sha...  15 us
    unnamed x29, local copies, waits for them, and re-layouts  8.76 us
    unnamed x1, blocking collectives  7.01 us
    ppermute x2, waiting for transfers between devices, from_behind(): return lax.ppermute(x, axis, [(i, (i + by) % count) for i in range(count)])  6.16 us
    ppermute x2, starting transfers between devices, from_behind(): return lax.ppermute(x, axis, [(i, (i + by) % count) for i in range(count)])  4.59 us
  transfers between devices with their start and end apart: 5, of which 4 were waited for; matrix products, arithmetic and copies ran while one was open for 7% of the time, Pallas kernels for 0%

commit v1 on v0

--- a/solution.py
+++ b/solution.py
@@ -39,8 +39,8 @@
 
 
 def block_kernel(heads, shift_ref, type_ref, x_ref, g_ref, low_ref, high_ref, aw_ref, ow_ref, table_ref,
-                 piece_ref, grad_aw_ref, grad_ow_ref, grad_bias_ref,
-                 xs, gs, proj, gproj, att, bias_a, bias_b, rel, table, sems):
+                 piece_ref, grad_w_ref, grad_bias_ref, kinds_ref,
+                 xs, gs, proj, gproj, att, bias_a, bias_b, rel, table, line, piece, sems):
     shift = shift_ref[0]
     wins = table.shape[0]
     width = x_ref.shape[-1]
@@ -70,12 +70,14 @@
     for copy in copies:
         copy.wait()
     rel[...] = jnp.zeros_like(rel)
+    line[...] = jnp.zeros_like(line)
+    kinds_ref[...] = jnp.full_like(kinds_ref, -1)
     for w in range(wins):
-        for k in range(WIN_LEVEL * WIN_LEVEL * WIN_LAT):
-            zi, zj, ai = k // (WIN_LEVEL * WIN_LAT), k // WIN_LAT % WIN_LEVEL, k % WIN_LAT
-            rel[zi * WIN_LAT + ai, w * heads:(w + 1) * heads, zj * part:(zj + 1) * part] = table[
-                w, :, k * part:(k + 1) * part
-            ]
+        line[w * heads:(w + 1) * heads, :table.shape[2]] = table[w]
+        kinds_ref[w * heads:(w + 1) * heads, :] = jnp.full((heads, kinds_ref.shape[1]), type_ref[w, 0], jnp.int32)
+    for k in range(WIN_LEVEL * WIN_LEVEL * WIN_LAT):
+        zi, zj, ai = k // (WIN_LEVEL * WIN_LAT), k // WIN_LAT % WIN_LEVEL, k % WIN_LAT
+        rel[zi * WIN_LAT + ai, :, zj * part:(zj + 1) * part] = line[:, k * part:(k + 1) * part]
     lanes = rel.shape[2]
     row = lax.broadcasted_iota(jnp.int32, (lanes, TOK), 0)
     key = lax.broadcasted_iota(jnp.int32, (lanes, TOK), 1)
@@ -138,11 +140,15 @@
     chunks, chunk = piece_ref.shape[0], piece_ref.shape[-1]
     for n in range(chunks):
         cols = slice(n * chunk, (n + 1) * chunk)
-        total = sum(dot(gproj[c], aw_ref[c, cols, :], NT) for c in range(3))
-        piece_ref[n] = total.reshape(lines, PAD, chunk)[:, :WIN_LON].astype(BF16)
-    for c in range(3):
-        grad_aw_ref[c] = dot(tokens, gproj[c], TN)
-    grad_ow_ref[...] = dot(att[...], grads, TN)
+        piece[:, :chunk] = sum(dot(gproj[c], aw_ref[c, cols, :], NT) for c in range(3))
+        for c in range(WIN_LON):
+            piece_ref[n, c] = piece[pl.ds(c, lines, stride=PAD), :][:, :chunk].astype(BF16)
+    grad_w = [dot(gproj[c], tokens, TN).astype(BF16) for c in range(3)]
+    grad_w.append(dot(att[...], grads, TN).astype(BF16))
+    shares, share = grad_w_ref.shape[0], grad_w_ref.shape[1]
+    grad_w = jnp.concatenate(grad_w, axis=0)
+    for j in range(shares):
+        grad_w_ref[j] = grad_w[j * share:(j + 1) * share]
 
     folded = jnp.zeros((ROWS * group, lanes), F32)
     for c in range(WIN_LON):
@@ -160,12 +166,12 @@
         two = (got - one.astype(F32)).astype(BF16)
         folded = folded + pltpu.roll(dot(one, spread, NT) + dot(two, spread, NT), place, 1)
     rel[...] = folded.reshape(ROWS, group, lanes)
-    for w in range(wins):
-        for k in range(WIN_LEVEL * WIN_LEVEL * WIN_LAT):
-            zi, zj, ai = k // (WIN_LEVEL * WIN_LAT), k // WIN_LAT % WIN_LEVEL, k % WIN_LAT
-            grad_bias_ref[w, :, k * part:(k + 1) * part] = rel[
-                zi * WIN_LAT + ai, w * heads:(w + 1) * heads, zj * part:(zj + 1) * part
-            ]
+    for k in range(WIN_LEVEL * WIN_LEVEL * WIN_LAT):
+        zi, zj, ai = k // (WIN_LEVEL * WIN_LAT), k // WIN_LAT % WIN_LEVEL, k % WIN_LAT
+        line[:, k * part:(k + 1) * part] = rel[zi * WIN_LAT + ai, :, zj * part:(zj + 1) * part]
+    strips, strip = grad_bias_ref.shape[0], grad_bias_ref.shape[2]
+    for j in range(strips):
+        grad_bias_ref[j] = line[:, j * strip:(j + 1) * strip].astype(BF16)
 
 
 def block_backward(features, grad_out, low, high, attend_weight, output_weight, bias_table, bias_type, shift):
@@ -175,6 +181,9 @@
     wins = levels // WIN_LEVEL
     lines = wins * ROWS
     chunks = lax.axis_size("head")
+    strips = lax.axis_size("lon")
+    shares = strips * lax.axis_size("lat")
+    strip = -(-rel_total // (128 * strips)) * 128
     vmem = pl.BlockSpec(memory_space=pltpu.VMEM)
     smem = pl.BlockSpec(memory_space=pltpu.SMEM)
     lanes = -(-ROWS * SPAN // 128) * 128
@@ -182,10 +191,10 @@
     return pl.pallas_call(
         functools.partial(block_kernel, heads),
         out_shape=(
-            jax.ShapeDtypeStruct((chunks, lines, WIN_LON, width // chunks), BF16),
-            jax.ShapeDtypeStruct(attend_weight.shape, F32),
-            jax.ShapeDtypeStruct(output_weight.shape, F32),
-            jax.ShapeDtypeStruct((wins, heads, rel_total), F32),
+            jax.ShapeDtypeStruct((chunks, WIN_LON, lines, width // chunks), BF16),
+            jax.ShapeDtypeStruct((shares, 4 * inner // shares, width), BF16),
+            jax.ShapeDtypeStruct((strips, PAD, strip), BF16),
+            jax.ShapeDtypeStruct((PAD, 128), jnp.int32),
         ),
         in_specs=[smem, smem, vmem, vmem, vmem, vmem, vmem, vmem, pl.BlockSpec(memory_space=pl.ANY)],
         out_specs=(vmem, vmem, vmem, vmem),
@@ -199,6 +208,8 @@
             pltpu.VMEM((TOK * PAD, 128), F32),
             pltpu.VMEM((ROWS, PAD, lanes), F32),
             pltpu.VMEM((wins, heads, rel_total), F32),
+            pltpu.VMEM((PAD, strips * strip), F32),
+            pltpu.VMEM((total, 128), F32),
             pltpu.SemaphoreType.DMA((wins,)),
         ],
         compiler_params=pltpu.CompilerParams(vmem_limit_bytes=50 * 1024 * 1024),
@@ -223,25 +234,203 @@
     return from_behind(low, "lon", -1), from_behind(high, "lon", 1)
 
 
+def exchange_kernel(shift_ref, piece_ref, w_ref, bias_ref, kinds_ref,
+                    own_ref, edge_ref, all_w_ref, all_bias_ref, all_kinds_ref,
+                    piece_in, w_in, bias_in, w_sum, bias_sum, edge_out, send, recv):
+    lons, lats, heads = (lax.axis_size(name) for name in ("lon", "lat", "head"))
+    lon, lat, head = (lax.axis_index(name) for name in ("lon", "lat", "head"))
+    mine = lon * lats + lat
+    pairs = [(a, b) for a in range(lons) for b in range(lats) if a or b]
+
+    def grid_peer(a, b):
+        return lax.rem(lon + a, lons), lax.rem(lat + b, lats)
+
+    def group_peer(n):
+        return lax.rem(head + n, heads)
+
+    barrier = pltpu.get_barrier_semaphore()
+    for a, b in pairs:
+        x, y = grid_peer(a, b)
+        pl.semaphore_signal(barrier, inc=1, device_id=(x, y, head), device_id_type=pl.DeviceIdType.MESH)
+    for n in range(1, heads):
+        pl.semaphore_signal(
+            barrier, inc=1, device_id=(lon, lat, group_peer(n)), device_id_type=pl.DeviceIdType.MESH
+        )
+    pl.semaphore_wait(barrier, len(pairs) + heads - 1)
+    count = [0]
+
+    def post(src, dst, device):
+        k = count[0]
+        count[0] += 1
+        copy = pltpu.make_async_remote_copy(
+            src_ref=src, dst_ref=dst, send_sem=send.at[k], recv_sem=recv.at[k],
+            device_id=device, device_id_type=pl.DeviceIdType.MESH,
+        )
+        copy.start()
+        return copy
+
+    bias_copies = []
+    for a in range(1, lons):
+        x, y = grid_peer(a, 0)
+        bias_copies.append(post(bias_ref.at[x], bias_in.at[a - 1], (x, y, head)))
+    w_copies = []
+    for i, (a, b) in enumerate(pairs):
+        x, y = grid_peer(a, b)
+        w_copies.append(post(w_ref.at[x * lats + y], w_in.at[i], (x, y, head)))
+    piece_copies = []
+    for n in range(1, heads):
+        to = group_peer(n)
+        piece_copies.append(post(piece_ref.at[to], piece_in.at[n - 1], (lon, lat, to)))
+    late = []
+    for b in range(1, lats):
+        x, y = grid_peer(0, b)
+        late.append(post(kinds_ref, all_kinds_ref.at[lat], (x, y, head)))
+    all_kinds_ref[pl.ds(lat, 1)] = kinds_ref[...][None]
+
+    for copy in bias_copies:
+        copy.wait_recv()
+    total = bias_ref[lon].astype(F32)
+    for a in range(lons - 1):
+        total = total + bias_in[a].astype(F32)
+    bias_sum[...] = total.astype(BF16)
+    all_bias_ref[pl.ds(mine, 1)] = total.astype(BF16)[None]
+    for a, b in pairs:
+        x, y = grid_peer(a, b)
+        late.append(post(bias_sum, all_bias_ref.at[mine], (x, y, head)))
+
+    for copy in w_copies:
+        copy.wait_recv()
+    total = w_ref[mine].astype(F32)
+    for i in range(len(pairs)):
+        total = total + w_in[i].astype(F32)
+    w_sum[...] = total.astype(BF16)
+    all_w_ref[pl.ds(mine, 1)] = total.astype(BF16)[None]
+    for a, b in pairs:
+        x, y = grid_peer(a, b)
+        late.append(post(w_sum, all_w_ref.at[mine], (x, y, head)))
+
+    for copy in piece_copies:
+        copy.wait_recv()
+    total = piece_ref[head].astype(F32)
+    for n in range(heads - 1):
+        total = total + piece_in[n].astype(F32)
+    own_ref[...] = total.astype(BF16)
+    if lons <= 2:
+        low = jnp.where(shift_ref[0] <= HALF, 1.0, 0.0)
+        edge_out[:HALF] = (total[:HALF] * low + total[HALF:] * (1.0 - low)).astype(BF16)
+    else:
+        edge_out[...] = total.astype(BF16)
+    sends = [(1, 0)] if lons <= 2 else [(1, 0), (lons - 1, HALF)]
+    for a, first in sends:
+        x, y = grid_peer(a, 0)
+        late.append(post(edge_out.at[pl.ds(first, HALF)], edge_ref.at[pl.ds(first, HALF)], (x, y, head)))
+    if lons <= 2:
+        edge_ref[HALF:] = jnp.zeros_like(edge_out[HALF:])
+    for copy in late:
+        copy.wait_recv()
+    for copy in bias_copies + w_copies + piece_copies + late:
+        copy.wait_send()
+
+
+def exchange(pieces, grad_w, grad_bias, kinds, shift):
+    lons, lats, heads = (lax.axis_size(name) for name in ("lon", "lat", "head"))
+    shares = lons * lats
+    vmem = pl.BlockSpec(memory_space=pltpu.VMEM)
+    copies = (lons - 1) + 3 * (shares - 1) + (heads - 1) + (lats - 1) + 2
+    return pl.pallas_call(
+        exchange_kernel,
+        out_shape=(
+            jax.ShapeDtypeStruct(pieces.shape[1:], BF16),
+            jax.ShapeDtypeStruct(pieces.shape[1:], BF16),
+            jax.ShapeDtypeStruct(grad_w.shape, BF16),
+            jax.ShapeDtypeStruct((shares, *grad_bias.shape[1:]), BF16),
+            jax.ShapeDtypeStruct((lats, *kinds.shape), jnp.int32),
+        ),
+        in_specs=[pl.BlockSpec(memory_space=pltpu.SMEM)] + [vmem] * 4,
+        out_specs=(vmem,) * 5,
+        scratch_shapes=[
+            pltpu.VMEM((heads - 1, *pieces.shape[1:]), BF16),
+            pltpu.VMEM((shares - 1, *grad_w.shape[1:]), BF16),
+            pltpu.VMEM((max(lons - 1, 1), *grad_bias.shape[1:]), BF16),
+            pltpu.VMEM(grad_w.shape[1:], BF16),
+            pltpu.VMEM(grad_bias.shape[1:], BF16),
+            pltpu.VMEM(pieces.shape[1:], BF16),
+            pltpu.SemaphoreType.DMA((copies,)),
+            pltpu.SemaphoreType.DMA((copies,)),
+        ],
+        compiler_params=pltpu.CompilerParams(
+            collective_id=0, has_side_effects=True, vmem_limit_bytes=50 * 1024 * 1024
+        ),
+    )(shift, pieces, grad_w, grad_bias, kinds)
+
+
+def finish_kernel(lats, shift_ref, own_ref, edge_ref, w_ref, bias_ref, kinds_ref,
+                  feature_ref, aw_ref, ow_ref, table_ref, wide):
+    shift = shift_ref[0]
+    cols, lines, chunk = own_ref.shape
+    for c in range(cols):
+        flag = use_neighbour(shift, c).astype(F32)
+        other = edge_ref[c % HALF] if lats[0] <= 2 else edge_ref[c]
+        mixed = other.astype(F32) * flag + own_ref[c].astype(F32) * (1.0 - flag)
+        wide[pl.ds(c, lines, stride=PAD), :] = jnp.concatenate(
+            [mixed, jnp.zeros((lines, 128 - chunk), F32)], axis=1
+        )
+    feature_ref[...] = wide[...].reshape(lines, PAD, 128)[:, :cols, :chunk].astype(BF16)
+    full = jnp.concatenate([w_ref[j].astype(F32) for j in range(w_ref.shape[0])], axis=0)
+    inner = full.shape[0] // 4
+    for c in range(3):
+        aw_ref[c] = full[c * inner:(c + 1) * inner].T
+    ow_ref[...] = full[3 * inner:]
+
+    rows = kinds_ref.shape[0] * kinds_ref.shape[1]
+    kinds = kinds_ref[...].reshape(rows, 128)
+    types, heads, total = table_ref.shape
+    held = lax.broadcasted_iota(jnp.int32, (rows, 128), 0) % kinds_ref.shape[1] % heads
+    lane = lax.broadcasted_iota(jnp.int32, (rows, 128), 1)
+    strip = bias_ref.shape[2]
+    for h in range(heads):
+        pick = ((kinds == lane) & (held == h)).astype(F32).astype(BF16)[:, :types]
+        for j in range(lats[0]):
+            wide_rows = jnp.concatenate(
+                [bias_ref[j * lats[1] + b] for b in range(lats[1])], axis=0
+            )
+            stop = min(total, (j + 1) * strip)
+            if stop > j * strip:
+                out = dot(pick, wide_rows, TN)
+                table_ref[:, h, j * strip:stop] = out[:, :stop - j * strip]
+
+
+def finish(own, edge, all_w, all_bias, all_kinds, shift, types, heads, rel_total):
+    cols, lines, chunk = own.shape
+    inner = all_w.shape[0] * all_w.shape[1] // 4
+    width = all_w.shape[2]
+    vmem = pl.BlockSpec(memory_space=pltpu.VMEM)
+    return pl.pallas_call(
+        functools.partial(finish_kernel, (lax.axis_size("lon"), lax.axis_size("lat"))),
+        out_shape=(
+            jax.ShapeDtypeStruct((lines, cols, chunk), BF16),
+            jax.ShapeDtypeStruct((3, width, inner), F32),
+            jax.ShapeDtypeStruct((inner, width), F32),
+            jax.ShapeDtypeStruct((types, heads, rel_total), F32),
+        ),
+        in_specs=[pl.BlockSpec(memory_space=pltpu.SMEM)] + [vmem] * 5,
+        out_specs=(vmem,) * 4,
+        scratch_shapes=[pltpu.VMEM((lines * PAD, 128), F32)],
+        compiler_params=pltpu.CompilerParams(vmem_limit_bytes=50 * 1024 * 1024),
+    )(shift, own, edge, all_w, all_bias, all_kinds)
+
+
 def per_device(features, attend_weight, output_weight, bias_table, bias_type, window_shift, grad_out):
     shift = window_shift[0]
     levels, lat_rows, lon_cols, width = features.shape
     stacked = jnp.stack((features, grad_out)).reshape(2, levels * lat_rows, lon_cols, width)
     low, high = swap_columns(stacked[:, :, :HALF], stacked[:, :, HALF:], shift)
-    pieces, grad_attend, grad_output, grad_bias = block_backward(
+    pieces, grad_w, grad_bias, kinds = block_backward(
         features, grad_out, low, high, attend_weight, output_weight, bias_table, bias_type, window_shift
     )
-    summed = lax.psum_scatter(pieces, "head", scatter_dimension=0, tiled=False)
-    low, high = swap_columns(summed[:, :HALF], summed[:, HALF:], shift)
-    taken = use_neighbour(shift, jnp.arange(lon_cols))[None, :, None]
-    feature_grad = jnp.where(taken, jnp.concatenate((low, high), axis=1), summed)
-    feature_grad = feature_grad.reshape(levels, lat_rows, lon_cols, -1)
-    attend_grad, output_grad = lax.psum((grad_attend, grad_output), ("lon", "lat"))
-    parts = lax.all_gather(grad_bias, ("lon", "lat")).reshape(-1, *bias_table.shape[1:])
-    types = lax.all_gather(bias_type[:, 0], ("lon", "lat")).reshape(-1)
-    selector = (types[:, None] == jnp.arange(bias_table.shape[0], dtype=jnp.int32)[None, :]).astype(F32)
-    bias_grad = jnp.einsum("at,ahr->thr", selector, parts, precision=lax.Precision.HIGHEST)
-    return (feature_grad, attend_grad, output_grad, bias_grad)
+    gathered = exchange(pieces, grad_w, grad_bias, kinds, window_shift)
+    feature_grad, attend_grad, output_grad, bias_grad = finish(*gathered, window_shift, *bias_table.shape)
+    return (feature_grad.reshape(levels, lat_rows, lon_cols, -1), attend_grad, output_grad, bias_grad)
 
 
 def solution(mesh):

time: 140 us -> 61.8 us (0.44)
  waiting for transfers between devices: 80 us -> 4.53 us
  Pallas kernels: 15 us -> 37 us
  between operations: 17 us -> 1.43 us
  blocking collectives: 7.01 us -> 0 us
  local copies, waits for them, and re-layouts: 9.26 us -> 15.3 us
  matrix products: 4.21 us -> 0 us
  other arithmetic: 2.77 us -> 0.06 us
  starting transfers between devices: 4.71 us -> 3.03 us
    psum x1 -> x0, waiting for transfers between devices: 26.2 us -> none  [per_device(): lax.psum((grad_attend, grad_output), ('lon', 'lat'))]
    all_gather x1 -> x0, waiting for transfers between devices: 24.2 us -> none  [per_device(): lax.all_gather(grad_bias, ('lon', 'lat')).reshape(-1, *bias_table.shape[1:])]
    pallas_call x0 -> x2, Pallas kernels: none -> 23 us  [the longest x1 20.1 us: exchange(): pl.pallas_call(exchange_kernel, out_shape=(jax.ShapeDtypeStruct(pieces.sh...]
    reduce_scatter x1 -> x0, waiting for transfers between devices: 22.3 us -> none  [per_device(): summed = lax.psum_scatter(pieces, 'head', scatter_dimension=0, tiled=False)]
    unnamed x1 -> x0, blocking collectives: 7.01 us -> none
    unnamed x29 -> x21, local copies, waits for them, and re-layouts: 8.76 us -> 13.8 us
    dot_general x1 -> x0, matrix products: 4.21 us -> none  [per_device(): jnp.einsum('at,ahr->thr', selector, parts, precision=lax.Precision.HIGHEST)]
    select_n x1 -> x0, other arithmetic: 1.68 us -> none  [per_device(): jnp.where(taken, jnp.concatenate((low, high), axis=1), summed)]
  transfers between devices with their start and end apart: 5 -> 1, of which waited for: 4 -> 1; matrix products, arithmetic and copies ran while one was open for 7% -> 9% of each run, Pallas kernels for 0% -> 0%
where the time goes in v1:
time: 61.8 us; the launch traced here: 61.4 us
  Pallas kernels  37 us (60%)
  local copies, waits for them, and re-layouts  15.3 us (25%)
  waiting for transfers between devices  4.53 us (7%)
  starting transfers between devices  3.03 us (5%)
  between operations  1.43 us (2%)
    pallas_call x1, Pallas kernels, exchange(): pl.pallas_call(exchange_kernel, out_shape=(jax.ShapeDtypeStruct(pieces.sh...  20.1 us
    pallas_call x1, Pallas kernels, block_backward(): pl.pallas_call(functools.partial(block_kernel, heads), out_shape=(jax.Sha...  14 us
    unnamed x21, local copies, waits for them, and re-layouts  13.8 us
    ppermute x1, waiting for transfers between devices, from_behind(): return lax.ppermute(x, axis, [(i, (i + by) % count) for i in range(count)])  4.53 us
    ppermute x1, starting transfers between devices, from_behind(): return lax.ppermute(x, axis, [(i, (i + by) % count) for i in range(count)])  3.03 us
    pallas_call x1, Pallas kernels, finish(): pl.pallas_call(functools.partial(finish_kernel, (lax.axis_size('lon'), la...  2.91 us
  transfers between devices with their start and end apart: 1, of which 1 were waited for; matrix products, arithmetic and copies ran while one was open for 9% of the time, Pallas kernels for 0%

profile of v1, /device:TPU:0, one launch (start us, length us, event | category | flops | bytes accessed | tf_op | source)
XLA Modules:
  0.0 61.4 jit_solution(10646557934253103647)
XLA Ops:
  1.3 0.0 copy-start.1
  1.3 1.2 %copy.35 = bf16[8,6,12,384]{3,1,0,2:T(8,128)(2,1)S(1)} copy(bf16[8,6,12,384]{3,0,2,1:T(8,128)(2,1)} %param.7) | data formatting | bytes 884736 | tf_op args[0]
  2.5 0.0 copy-start.2
  2.5 0.1 stack.9
  2.7 0.0 copy-start.4
  2.7 0.0 copy-start.3
  2.8 1.2 %copy.36 = bf16[8,6,12,384]{3,1,0,2:T(8,128)(2,1)S(1)} copy(bf16[8,6,12,384]{3,0,2,1:T(8,128)(2,1)} %param.13) | data formatting | bytes 884736 | tf_op args[6]
  4.0 0.1 stack.10
  4.1 0.1 constant_dynamic-update-slice_fusion
  4.2 0.1 slice_select_fusion
  4.3 3.0 %collective-permute-start = (bf16[2,48,6,384]{3,1,2,0:T(8,128)(2,1)S(1)}, bf16[2,48,6,384]{3,1,2,0:T(8,128)(2,1)}, u32[]{:S(2)}, u32[]{:S(2)}) collective-permute-start(bf16[2,48,6,384]{3,1,2,0:T(8,128)(2,1)S(1)} %slice_select_fusion), channel_id=1, source_target_pairs={{0,16},{16,0},{1,17},{17,1},{2,18},{18,2},{3,19},{19,3},{4,20},{20... | collective-permute-start | bytes 1327112 | tf_op jit(solution)/shard_map/ppermute | solution.py:24
  7.3 0.0 copy-done.1
  7.3 0.1 copy.33
  7.4 0.0 copy-done.2
  7.4 0.1 copy.34
  7.5 0.0 copy-done.4
  7.5 0.1 copy.37.type_ref
  7.6 0.0 copy-done.3
  7.6 0.2 copy.40.aw_ref
  7.8 0.0 copy-start
  7.8 5.2 %copy.41.table_ref = f32[64,3,3312]{2,1,0:T(4,128)} copy(f32[64,3,3312]{2,0,1:T(8,128)} %param.10) | data formatting | bytes 5087232 | tf_op args[3]
  13.1 4.5 %collective-permute-done = bf16[2,48,6,384]{3,1,2,0:T(8,128)(2,1)} collective-permute-done((bf16[2,48,6,384]{3,1,2,0:T(8,128)(2,1)S(1)}, bf16[2,48,6,384]{3,1,2,0:T(8,128)(2,1)}, u32[]{:S(2)}, u32[]{:S(2)}) %collective-permute-start) | collective-permute-done | bytes 442400 | tf_op jit(solution)/shard_map/ppermute | solution.py:24
  17.6 1.1 %copy.38.low_ref.high_ref = bf16[2,48,6,384]{3,2,1,0:T(8,128)(2,1)S(1)} copy(bf16[2,48,6,384]{3,1,2,0:T(8,128)(2,1)} %collective-permute-done) | data formatting | bytes 884736 | tf_op jit(solution)/shard_map/ppermute | solution.py:24
  18.7 0.0 copy-done
  18.7 14.0 %shard_map.102 = (bf16[4,12,48,96]{3,2,1,0:T(8,128)(2,1)S(1)}, bf16[8,48,384]{2,1,0:T(8,128)(2,1)S(1)}, bf16[2,16,1664]{2,1,0:T(8,128)(2,1)S(1)}, s32[16,128]{1,0:T(8,128)S(1)}) custom-call(s32[1]{0:T(128)S(6)} %copy.46.shift_ref, s32[4,1]{1,0:T(4,128)S(1)} %copy.37.type_ref, bf16[48,12,384]{2,1,0:T(8,128)(2,1)S(1)} %bitcast.8, ...), custom_call_target="tpu_custom_call" | custom-call | flops 1000000000 | bytes 10000000 | tf_op jit(solution)/shard_map/pallas_call | solution.py:191
  32.7 20.1 %shard_map.103 = (bf16[12,48,96]{2,1,0:T(8,128)(2,1)S(1)}, bf16[12,48,96]{2,1,0:T(8,128)(2,1)S(1)}, bf16[8,48,384]{2,1,0:T(8,128)(2,1)S(1)}, bf16[8,16,1664]{2,1,0:T(8,128)(2,1)S(1)}, s32[4,16,128]{2,1,0:T(8,128)S(1)}) custom-call(s32[1]{0:T(128)S(6)} %copy.46.shift_ref, bf16[4,12,48,96]{3,2,1,0:T(8,128)(2,1)S(1)} %get-tuple-element.17.piece_ref, ...), custom_call_target="tpu_custom_call" | custom-call | tf_op jit(solution)/shard_map/pallas_call | solution.py:340
  52.9 2.9 %shard_map.104 = (bf16[48,12,96]{2,1,0:T(8,128)(2,1)S(1)}, f32[3,384,96]{2,1,0:T(8,128)S(1)}, f32[96,384]{1,0:T(8,128)}, f32[64,3,3312]{2,1,0:T(4,128)}) custom-call(s32[1]{0:T(128)S(6)} %copy.46.shift_ref, bf16[12,48,96]{2,1,0:T(8,128)(2,1)S(1)} %get-tuple-element.21.own_ref, bf16[12,48,96]{2,1,0:T(8,128)(2,1)S(1)} %get-tuple-element.22.edge_ref, ...), custom_call_target="tpu_custom_call" | custom-call | tf_op jit(solution)/shard_map/pallas_call | solution.py:408
  55.8 0.7 %copy.42 = bf16[8,6,12,96]{3,0,2,1:T(8,128)(2,1)} copy(bf16[8,6,12,96]{3,2,1,0:T(8,128)(2,1)S(1)} %bitcast.10) | data formatting | bytes 221184
  56.5 1.0 %copy.43 = f32[3,384,96]{1,2,0:T(8,128)} copy(f32[3,384,96]{2,1,0:T(8,128)S(1)} %get-tuple-element.39) | data formatting | bytes 884736
  57.5 3.9 %copy.44 = f32[64,3,3312]{2,0,1:T(8,128)} copy(f32[64,3,3312]{2,1,0:T(4,128)} %get-tuple-element.41) | data formatting | bytes 5087232
  (1 shorter events, 0.0 us)
Async XLA Ops:
  1.3 6.0 %copy-start.1 = (bf16[8,6,12,384]{3,0,2,1:T(8,128)(2,1)S(1)}, bf16[8,6,12,384]{3,0,2,1:T(8,128)(2,1)}, u32[]{:S(2)}) copy-start(bf16[8,6,12,384]{3,0,2,1:T(8,128)(2,1)} %param.7) | copy-start | bytes 1327108
  2.5 4.9 %copy-start.2 = (bf16[8,6,12,384]{3,0,2,1:T(8,128)(2,1)S(1)}, bf16[8,6,12,384]{3,0,2,1:T(8,128)(2,1)}, u32[]{:S(2)}) copy-start(bf16[8,6,12,384]{3,0,2,1:T(8,128)(2,1)} %param.13) | copy-start | bytes 1327108
  2.7 4.8 %copy-start.4 = (s32[4,1]{0,1:T(1,128)S(1)}, s32[4,1]{0,1:T(1,128)}, u32[]{:S(2)}) copy-start(s32[4,1]{0,1:T(1,128)} %param.11) | copy-start | bytes 52
  2.7 4.9 %copy-start.3 = (bf16[3,384,96]{1,2,0:T(8,128)(2,1)S(1)}, bf16[3,384,96]{1,2,0:T(8,128)(2,1)}, u32[]{:S(2)}) copy-start(bf16[3,384,96]{1,2,0:T(8,128)(2,1)} %param.8) | copy-start | bytes 663556
  4.3 13.3 %collective-permute-start = (bf16[2,48,6,384]{3,1,2,0:T(8,128)(2,1)S(1)}, bf16[2,48,6,384]{3,1,2,0:T(8,128)(2,1)}, u32[]{:S(2)}, u32[]{:S(2)}) collective-permute-start(bf16[2,48,6,384]{3,1,2,0:T(8,128)(2,1)S(1)} %slice_select_fusion), channel_id=1, source_target_pairs={{0,16},{16,0},{1,17},{17,1},{2,18},{18,2},{3,19},{19,3},{4,20},{20... | collective-permute-start | bytes 1327112 | tf_op jit(solution)/shard_map/ppermute | solution.py:24
  7.8 10.9 %copy-start = (bf16[96,384]{1,0:T(8,128)(2,1)S(1)}, bf16[96,384]{1,0:T(8,128)(2,1)}, u32[]{:S(2)}) copy-start(bf16[96,384]{1,0:T(8,128)(2,1)} %ow_ref.1) | copy-start | bytes 221188

commit v2 on v1

--- a/solution.py
+++ b/solution.py
@@ -38,34 +38,25 @@
     return (col >= first) & (col < jnp.where(shift <= HALF, shift, WIN_LON))
 
 
-def block_kernel(heads, shift_ref, type_ref, x_ref, g_ref, low_ref, high_ref, aw_ref, ow_ref, table_ref,
-                 piece_ref, grad_w_ref, grad_bias_ref, kinds_ref,
-                 xs, gs, proj, gproj, att, bias_a, bias_b, rel, table, line, piece, sems):
+def spread_matrix(lanes, shift):
+    row = lax.broadcasted_iota(jnp.int32, (lanes, TOK), 0)
+    key = lax.broadcasted_iota(jnp.int32, (lanes, TOK), 1)
+    slot = key % PAD
+    pos = slot + WIN_LON - shift
+    pos = jnp.where(pos >= WIN_LON, pos - WIN_LON, pos)
+    hit = (row == key // PAD * SPAN + WIN_LON - 1 - pos) & (slot < WIN_LON)
+    return jnp.where(hit, 1.0, 0.0).astype(BF16)
+
+
+def bias_kernel(heads, shift_ref, type_ref, table_ref, bias_a, bias_b, kinds_ref, rel, table, line, sems):
     shift = shift_ref[0]
     wins = table.shape[0]
-    width = x_ref.shape[-1]
-    inner = aw_ref.shape[2]
-    size = inner // heads
     part = WIN_LAT * SPAN
     copies = [
         pltpu.make_async_copy(table_ref.at[type_ref[w, 0]], table.at[w], sems.at[w]) for w in range(wins)
     ]
     for copy in copies:
         copy.start()
-
-    lines = wins * ROWS
-    col = lax.broadcasted_iota(jnp.int32, (lines, WIN_LON, width), 1)
-    taken = use_neighbour(shift, col)
-    for src, dst, n in ((x_ref, xs, 0), (g_ref, gs, 1)):
-        near = jnp.concatenate([low_ref[n].astype(F32), high_ref[n].astype(F32)], axis=1)
-        picked = jnp.where(taken, near, src[...].astype(F32))
-        full = jnp.concatenate([picked, jnp.zeros((lines, PAD - WIN_LON, width), F32)], axis=1)
-        dst[...] = full.astype(BF16).reshape(lines * PAD, width)
-    tokens = xs[...]
-    grads = gs[...]
-    for c in range(3):
-        proj[c] = dot(tokens, aw_ref[c], NN).astype(BF16)
-    proj[3] = dot(grads, ow_ref[...], NT).astype(BF16)
 
     for copy in copies:
         copy.wait()
@@ -79,13 +70,7 @@
         zi, zj, ai = k // (WIN_LEVEL * WIN_LAT), k // WIN_LAT % WIN_LEVEL, k % WIN_LAT
         rel[zi * WIN_LAT + ai, :, zj * part:(zj + 1) * part] = line[:, k * part:(k + 1) * part]
     lanes = rel.shape[2]
-    row = lax.broadcasted_iota(jnp.int32, (lanes, TOK), 0)
-    key = lax.broadcasted_iota(jnp.int32, (lanes, TOK), 1)
-    slot = key % PAD
-    pos = slot + WIN_LON - shift
-    pos = jnp.where(pos >= WIN_LON, pos - WIN_LON, pos)
-    hit = (row == key // PAD * SPAN + WIN_LON - 1 - pos) & (slot < WIN_LON)
-    spread = jnp.where(hit, 1.0, 0.0).astype(BF16)
+    spread = spread_matrix(lanes, shift)
     unused = jnp.where(lax.broadcasted_iota(jnp.int32, (1, TOK), 1) % PAD < WIN_LON, 0.0, -1e30)
     group = PAD
     flat = rel[...].reshape(ROWS * group, lanes)
@@ -105,6 +90,60 @@
             bias_a[base:base + group, :] = out[p * group:(p + 1) * group, :128]
             bias_b[base:base + group, :TOK - 128] = out[p * group:(p + 1) * group, 128:]
 
+
+def spread_bias(bias_table, bias_type, shift):
+    heads, rel_total = bias_table.shape[1:]
+    wins = bias_type.shape[0]
+    vmem = pl.BlockSpec(memory_space=pltpu.VMEM)
+    smem = pl.BlockSpec(memory_space=pltpu.SMEM)
+    lanes = -(-ROWS * SPAN // 128) * 128
+    return pl.pallas_call(
+        functools.partial(bias_kernel, heads),
+        out_shape=(
+            jax.ShapeDtypeStruct((TOK * PAD, 128), F32),
+            jax.ShapeDtypeStruct((TOK * PAD, 128), F32),
+            jax.ShapeDtypeStruct((PAD, 128), jnp.int32),
+        ),
+        in_specs=[smem, smem, pl.BlockSpec(memory_space=pl.ANY)],
+        out_specs=(vmem,) * 3,
+        scratch_shapes=[
+            pltpu.VMEM((ROWS, PAD, lanes), F32),
+            pltpu.VMEM((wins, heads, rel_total), F32),
+            pltpu.VMEM((PAD, -(-rel_total // 128) * 128), F32),
+            pltpu.SemaphoreType.DMA((wins,)),
+        ],
+        compiler_params=pltpu.CompilerParams(vmem_limit_bytes=20 * 1024 * 1024),
+        cost_estimate=pl.CostEstimate(flops=5 * 10**8, bytes_accessed=4 * 10**6, transcendentals=0),
+    )(shift, bias_type, bias_table)
+
+
+def block_kernel(heads, shift_ref, x_ref, g_ref, low_ref, high_ref, aw_ref, ow_ref, from_a, from_b,
+                 piece_ref, grad_w_ref, grad_bias_ref,
+                 xs, gs, proj, gproj, att, bias_a, bias_b, rel, line, piece):
+    shift = shift_ref[0]
+    wins = x_ref.shape[0] // ROWS
+    width = x_ref.shape[-1]
+    inner = aw_ref.shape[2]
+    size = inner // heads
+    part = WIN_LAT * SPAN
+    lines = wins * ROWS
+    col = lax.broadcasted_iota(jnp.int32, (lines, WIN_LON, width), 1)
+    taken = use_neighbour(shift, col)
+    for src, dst, n in ((x_ref, xs, 0), (g_ref, gs, 1)):
+        near = jnp.concatenate([low_ref[n].astype(F32), high_ref[n].astype(F32)], axis=1)
+        picked = jnp.where(taken, near, src[...].astype(F32))
+        full = jnp.concatenate([picked, jnp.zeros((lines, PAD - WIN_LON, width), F32)], axis=1)
+        dst[...] = full.astype(BF16).reshape(lines * PAD, width)
+    tokens = xs[...]
+    grads = gs[...]
+    for c in range(3):
+        proj[c] = dot(tokens, aw_ref[c], NN).astype(BF16)
+    proj[3] = dot(grads, ow_ref[...], NT).astype(BF16)
+
+    spread = spread_matrix(rel.shape[2], shift)
+    lanes = rel.shape[2]
+    group = PAD
+
     scaling = size ** -0.5
     lane = lax.broadcasted_iota(jnp.int32, (TOK, inner), 1) // size
     for w in range(wins):
@@ -116,7 +155,7 @@
             mine = (lane == h).astype(BF16)
             qh, kh, vh, gah = q * mine, k * mine, v * mine, ga * mine
             rows = pl.ds(e, TOK, stride=group)
-            bias = jnp.concatenate([bias_a[rows, :], bias_b[rows, :][:, :TOK - 128]], axis=1)
+            bias = jnp.concatenate([from_a[rows, :], from_b[rows, :][:, :TOK - 128]], axis=1)
             scores = dot(qh, k, NT) * scaling + bias
             top = jnp.max(scores, axis=1, keepdims=True)
             raised = jnp.exp(scores - top)
@@ -150,6 +189,7 @@
     for j in range(shares):
         grad_w_ref[j] = grad_w[j * share:(j + 1) * share]
 
+    line[...] = jnp.zeros_like(line)
     folded = jnp.zeros((ROWS * group, lanes), F32)
     for c in range(WIN_LON):
         place = lax.rem(c + WIN_LON - shift, WIN_LON)
@@ -171,12 +211,13 @@
         line[:, k * part:(k + 1) * part] = rel[zi * WIN_LAT + ai, :, zj * part:(zj + 1) * part]
     strips, strip = grad_bias_ref.shape[0], grad_bias_ref.shape[2]
     for j in range(strips):
-        grad_bias_ref[j] = line[:, j * strip:(j + 1) * strip].astype(BF16)
-
-
-def block_backward(features, grad_out, low, high, attend_weight, output_weight, bias_table, bias_type, shift):
+        used = lax.broadcasted_iota(jnp.int32, (PAD, strip), 0) < wins * heads
+        grad_bias_ref[j] = jnp.where(used, line[:, j * strip:(j + 1) * strip], 0.0).astype(BF16)
+
+
+def block_backward(features, grad_out, low, high, attend_weight, output_weight, bias, table_shape, shift):
     levels, lat_rows, lon_cols, width = features.shape
-    heads, rel_total = bias_table.shape[1:]
+    heads, rel_total = table_shape[1:]
     inner = attend_weight.shape[2]
     wins = levels // WIN_LEVEL
     lines = wins * ROWS
@@ -194,10 +235,9 @@
             jax.ShapeDtypeStruct((chunks, WIN_LON, lines, width // chunks), BF16),
             jax.ShapeDtypeStruct((shares, 4 * inner // shares, width), BF16),
             jax.ShapeDtypeStruct((strips, PAD, strip), BF16),
-            jax.ShapeDtypeStruct((PAD, 128), jnp.int32),
         ),
-        in_specs=[smem, smem, vmem, vmem, vmem, vmem, vmem, vmem, pl.BlockSpec(memory_space=pl.ANY)],
-        out_specs=(vmem, vmem, vmem, vmem),
+        in_specs=[smem] + [vmem] * 8,
+        out_specs=(vmem,) * 3,
         scratch_shapes=[
             pltpu.VMEM((total, width), BF16),
             pltpu.VMEM((total, width), BF16),
@@ -207,23 +247,20 @@
             pltpu.VMEM((TOK * PAD, 128), F32),
             pltpu.VMEM((TOK * PAD, 128), F32),
             pltpu.VMEM((ROWS, PAD, lanes), F32),
-            pltpu.VMEM((wins, heads, rel_total), F32),
             pltpu.VMEM((PAD, strips * strip), F32),
             pltpu.VMEM((total, 128), F32),
-            pltpu.SemaphoreType.DMA((wins,)),
         ],
         compiler_params=pltpu.CompilerParams(vmem_limit_bytes=50 * 1024 * 1024),
         cost_estimate=pl.CostEstimate(flops=10**9, bytes_accessed=10**7, transcendentals=10**6),
     )(
         shift,
-        bias_type,
         features.reshape(lines, lon_cols, width),
         grad_out.reshape(lines, lon_cols, width),
         low,
         high,
         attend_weight,
         output_weight,
-        bias_table,
+        *bias,
     )
 
 
@@ -372,19 +409,19 @@
         flag = use_neighbour(shift, c).astype(F32)
         other = edge_ref[c % HALF] if lats[0] <= 2 else edge_ref[c]
         mixed = other.astype(F32) * flag + own_ref[c].astype(F32) * (1.0 - flag)
-        wide[pl.ds(c, lines, stride=PAD), :] = jnp.concatenate(
-            [mixed, jnp.zeros((lines, 128 - chunk), F32)], axis=1
-        )
-    feature_ref[...] = wide[...].reshape(lines, PAD, 128)[:, :cols, :chunk].astype(BF16)
+        wide[c * lines:(c + 1) * lines, :chunk] = mixed
+        for a in range(WIN_LAT):
+            levels = wide[pl.ds(c * lines + a, lines // WIN_LAT, stride=WIN_LAT), :]
+            feature_ref[a, c] = levels[:, :chunk].astype(BF16)
     full = jnp.concatenate([w_ref[j].astype(F32) for j in range(w_ref.shape[0])], axis=0)
     inner = full.shape[0] // 4
     for c in range(3):
-        aw_ref[c] = full[c * inner:(c + 1) * inner].T
+        aw_ref[c] = full[c * inner:(c + 1) * inner]
     ow_ref[...] = full[3 * inner:]
 
     rows = kinds_ref.shape[0] * kinds_ref.shape[1]
     kinds = kinds_ref[...].reshape(rows, 128)
-    types, heads, total = table_ref.shape
+    heads, types, total = table_ref.shape
     held = lax.broadcasted_iota(jnp.int32, (rows, 128), 0) % kinds_ref.shape[1] % heads
     lane = lax.broadcasted_iota(jnp.int32, (rows, 128), 1)
     strip = bias_ref.shape[2]
@@ -397,7 +434,7 @@
             stop = min(total, (j + 1) * strip)
             if stop > j * strip:
                 out = dot(pick, wide_rows, TN)
-                table_ref[:, h, j * strip:stop] = out[:, :stop - j * strip]
+                table_ref[h, :, j * strip:stop] = out[:, :stop - j * strip]
 
 
 def finish(own, edge, all_w, all_bias, all_kinds, shift, types, heads, rel_total):
@@ -408,14 +445,14 @@
     return pl.pallas_call(
         functools.partial(finish_kernel, (lax.axis_size("lon"), lax.axis_size("lat"))),
         out_shape=(
-            jax.ShapeDtypeStruct((lines, cols, chunk), BF16),
-            jax.ShapeDtypeStruct((3, width, inner), F32),
+            jax.ShapeDtypeStruct((WIN_LAT, cols, lines // WIN_LAT, chunk), BF16),
+            jax.ShapeDtypeStruct((3, inner, width), F32),
             jax.ShapeDtypeStruct((inner, width), F32),
-            jax.ShapeDtypeStruct((types, heads, rel_total), F32),
+            jax.ShapeDtypeStruct((heads, types, rel_total), F32),
         ),
         in_specs=[pl.BlockSpec(memory_space=pltpu.SMEM)] + [vmem] * 5,
         out_specs=(vmem,) * 4,
-        scratch_shapes=[pltpu.VMEM((lines * PAD, 128), F32)],
+        scratch_shapes=[pltpu.VMEM((lines * cols, 128), F32)],
         compiler_params=pltpu.CompilerParams(vmem_limit_bytes=50 * 1024 * 1024),
     )(shift, own, edge, all_w, all_bias, all_kinds)
 
@@ -423,14 +460,26 @@
 def per_device(features, attend_weight, output_weight, bias_table, bias_type, window_shift, grad_out):
     shift = window_shift[0]
     levels, lat_rows, lon_cols, width = features.shape
-    stacked = jnp.stack((features, grad_out)).reshape(2, levels * lat_rows, lon_cols, width)
-    low, high = swap_columns(stacked[:, :, :HALF], stacked[:, :, HALF:], shift)
-    pieces, grad_w, grad_bias, kinds = block_backward(
-        features, grad_out, low, high, attend_weight, output_weight, bias_table, bias_type, window_shift
-    )
+    stored = [x.transpose(1, 2, 0, 3) for x in (features, grad_out)]
+    low, high = swap_columns(
+        jnp.stack([x[:, :HALF] for x in stored]), jnp.stack([x[:, HALF:] for x in stored]), shift
+    )
+    bias = spread_bias(bias_table, bias_type, window_shift)
+    low, high = (
+        x.transpose(0, 3, 1, 2, 4).reshape(2, levels * lat_rows, HALF, width) for x in (low, high)
+    )
+    pieces, grad_w, grad_bias = block_backward(
+        features, grad_out, low, high, attend_weight, output_weight, bias[:2], bias_table.shape, window_shift
+    )
+    kinds = bias[2]
     gathered = exchange(pieces, grad_w, grad_bias, kinds, window_shift)
     feature_grad, attend_grad, output_grad, bias_grad = finish(*gathered, window_shift, *bias_table.shape)
-    return (feature_grad.reshape(levels, lat_rows, lon_cols, -1), attend_grad, output_grad, bias_grad)
+    return (
+        feature_grad.transpose(2, 0, 1, 3),
+        attend_grad.transpose(0, 2, 1),
+        output_grad,
+        bias_grad.transpose(1, 0, 2),
+    )
 
 
 def solution(mesh):

time: 61.8 us -> 53.1 us (0.86)
  local copies, waits for them, and re-layouts: 15.3 us -> 10.4 us
  waiting for transfers between devices: 4.53 us -> 0.01 us
  other arithmetic: 0.06 us -> 0.85 us
    unnamed x21 -> x25, local copies, waits for them, and re-layouts: 13.8 us -> 7.82 us
    ppermute x1, waiting for transfers between devices: 4.53 us -> 0.01 us  [from_behind(): return lax.ppermute(x, axis, [(i, (i + by) % count) for i in range(count)])]
    pallas_call x0 -> x1, Pallas kernels: none -> 3.55 us  [spread_bias(): pl.pallas_call(functools.partial(bias_kernel, heads), out_shape=(jax.Shap...]
    pallas_call x1, Pallas kernels: 14 us -> 11.6 us  [block_backward(): pl.pallas_call(functools.partial(block_kernel, heads), out_shape=(jax.Sha...]
    another operation x3 -> x1, local copies, waits for them, and re-layouts: 0.37 us -> 1.5 us  [per_device(): jnp.stack([x[:, HALF:] for x in stored])]
    ppermute x1 -> x0, local copies, waits for them, and re-layouts: 1.13 us -> none  [from_behind(): return lax.ppermute(x, axis, [(i, (i + by) % count) for i in range(count)])]
    transpose x0 -> x1, local copies, waits for them, and re-layouts: none -> 1.1 us  [per_device(): x.transpose(0, 3, 1, 2, 4).reshape(2, levels * lat_rows, HALF, width)]
    select_n x1, other arithmetic: 0.06 us -> 0.85 us  [swap_columns(): got = from_behind(jnp.where(shift <= HALF, low, high), 'lon', 1)]
  transfers between devices with their start and end apart: 1 -> 1, of which waited for: 1 -> 0; matrix products, arithmetic and copies ran while one was open for 9% -> 10% of each run, Pallas kernels for 0% -> 7%
where the time goes in v2:
time: 53.1 us; the launch traced here: 52.8 us
  Pallas kernels  37.1 us (70%)
  local copies, waits for them, and re-layouts  10.4 us (20%)
  starting transfers between devices  2.97 us (6%)
  between operations  1.47 us (3%)
  other arithmetic  0.85 us (2%)
    pallas_call x1, Pallas kernels, exchange(): pl.pallas_call(exchange_kernel, out_shape=(jax.ShapeDtypeStruct(pieces.sh...  19.7 us
    pallas_call x1, Pallas kernels, block_backward(): pl.pallas_call(functools.partial(block_kernel, heads), out_shape=(jax.Sha...  11.6 us
    unnamed x25, local copies, waits for them, and re-layouts  7.82 us
    pallas_call x1, Pallas kernels, spread_bias(): pl.pallas_call(functools.partial(bias_kernel, heads), out_shape=(jax.Shap...  3.55 us
    ppermute x1, starting transfers between devices, from_behind(): return lax.ppermute(x, axis, [(i, (i + by) % count) for i in range(count)])  2.97 us
    pallas_call x1, Pallas kernels, finish(): pl.pallas_call(functools.partial(finish_kernel, (lax.axis_size('lon'), la...  2.2 us
    another operation x1, local copies, waits for them, and re-layouts, per_device(): jnp.stack([x[:, HALF:] for x in stored])  1.5 us
    transpose x1, local copies, waits for them, and re-layouts, per_device(): x.transpose(0, 3, 1, 2, 4).reshape(2, levels * lat_rows, HALF, width)  1.1 us
  transfers between devices with their start and end apart: 1, of which 0 were waited for; matrix products, arithmetic and copies ran while one was open for 10% of the time, Pallas kernels for 7%

profile of v2, /device:TPU:0, one launch (start us, length us, event | category | flops | bytes accessed | tf_op | source)
XLA Modules:
  0.0 52.8 jit_solution(14951088875869269423)
XLA Ops:
  0.6 0.0 copy-start.7
  0.6 0.0 copy-start.8
  1.4 0.0 copy-start.6
  1.4 1.5 %slice_bitcast_fusion = (bf16[1,6,6,8,384]{4,3,2,1,0:T(8,128)(2,1)S(1)}, bf16[1,6,6,8,384]{4,3,2,1,0:T(8,128)(2,1)S(1)}, bf16[1,6,6,8,384]{4,3,2,1,0:T(8,128)(2,1)S(1)}, bf16[1,6,6,8,384]{4,3,2,1,0:T(8,128)(2,1)S(1)}) fusion(bf16[6,12,8,384]{3,2,1,0:T(8,128)(2,1)} %bitcast.23, bf16[6,12,8,384]{3,2,1,0:T(8,128)(2,1)} %bitcast.22), kind=kLoop, calls=%fused_computation.1 | loop fusion | bytes 1769472 | tf_op jit(solution)/shard_map/stack | solution.py:465
  2.9 0.9 %maximum_select_fusion = bf16[2,6,6,8,384]{4,3,2,1,0:T(8,128)(2,1)} fusion(bf16[1,6,6,8,384]{4,3,2,1,0:T(8,128)(2,1)S(1)} %get-tuple-element.37, bf16[1,6,6,8,384]{4,3,2,1,0:T(8,128)(2,1)S(1)} %get-tuple-element.38, bf16[1,6,6,8,384]{4,3,2,1,0:T(8,128)(2,1)S(1)} %get-tuple-element.36, bf16[1,6,6,8,384]{4,3,2,1,0:T(8,128)(2,1)S(1)} %get-tuple-element.39, pred[]{:T(512)} %bitcast.2), kind=kLoop, calls=%fused_computation | loop fusion | flops 663552 | bytes 1327105 | tf_op jit(solution)/shard_map/jit(_where)/select_n | solution.py:269
  3.7 3.0 %collective-permute-start = (bf16[2,6,6,8,384]{4,3,2,1,0:T(8,128)(2,1)}, bf16[2,6,6,8,384]{4,3,2,1,0:T(8,128)(2,1)}, u32[]{:S(2)}, u32[]{:S(2)}) collective-permute-start(bf16[2,6,6,8,384]{4,3,2,1,0:T(8,128)(2,1)} %maximum_select_fusion), channel_id=1, source_target_pairs={{0,16},{16,0},{1,17},{17,1},{2,18},{18,2},{3,19},{19,3},{4,20},{20... | collective-permute-start | bytes 1327112 | tf_op jit(solution)/shard_map/ppermute | solution.py:24
  6.7 0.0 copy-done.7
  6.7 0.9 %copy.11 = bf16[8,6,12,384]{3,2,1,0:T(8,128)(2,1)} copy(bf16[8,6,12,384]{3,0,2,1:T(8,128)(2,1)S(1)} %copy-done.7) | data formatting | bytes 884736 | tf_op args[0]
  7.6 0.0 copy-done.8
  7.6 0.9 %copy.12 = bf16[8,6,12,384]{3,2,1,0:T(8,128)(2,1)} copy(bf16[8,6,12,384]{3,0,2,1:T(8,128)(2,1)S(1)} %copy-done.8) | data formatting | bytes 884736 | tf_op args[6]
  8.5 0.0 copy-done.6
  8.5 0.0 copy-start.9
  8.5 1.8 %copy.15.table_ref = f32[64,3,3312]{2,1,0:T(4,128)S(1)} copy(f32[64,3,3312]{2,0,1:T(8,128)S(1)} %copy-done.6) | data formatting | bytes 5087232 | tf_op args[3]
  10.3 0.0 copy-done.9
  10.3 0.0 copy-start.5
  10.3 0.1 copy.14.type_ref
  10.4 1.8 %copy.16.aw_ref = bf16[3,384,96]{2,1,0:T(8,128)(2,1)} copy(bf16[3,384,96]{1,2,0:T(8,128)(2,1)} %param.8) | data formatting | bytes 442368 | tf_op args[1]
  12.2 0.0 copy-start
  12.2 0.0 copy-start.1
  12.2 0.0 copy-start.4
  12.2 3.5 %shard_map.102 = (f32[3072,128]{1,0:T(8,128)S(1)}, f32[3072,128]{1,0:T(8,128)S(1)}, s32[16,128]{1,0:T(8,128)S(1)}) custom-call(s32[1]{0:T(128)S(6)} %copy.17.shift_ref, s32[4,1]{1,0:T(4,128)S(1)} %copy.14.type_ref, f32[64,3,3312]{2,1,0:T(4,128)S(1)} %copy.15.table_ref), custom_call_target="tpu_custom_call" | custom-call | flops 500000000 | bytes 4000000 | tf_op jit(solution)/shard_map/pallas_call | solution.py:100
  15.8 0.0 copy-start.2
  15.8 1.1 %copy-done.2 = f32[3072,128]{1,0:T(8,128)} copy-done((f32[3072,128]{1,0:T(8,128)}, f32[3072,128]{1,0:T(8,128)S(1)}, u32[]{:S(2)}) %copy-start.2) | copy-done | bytes 1572888
  16.9 0.0 copy-start.3
  16.9 1.2 %copy-done.3 = f32[3072,128]{1,0:T(8,128)} copy-done((f32[3072,128]{1,0:T(8,128)}, f32[3072,128]{1,0:T(8,128)S(1)}, u32[]{:S(2)}) %copy-start.3) | copy-done | bytes 1572888
  18.1 0.0 collective-permute-done
  18.1 1.1 %copy.13 = bf16[2,8,6,6,384]{4,3,2,1,0:T(8,128)(2,1)S(1)} copy(bf16[2,8,6,6,384]{4,1,3,2,0:T(8,128)(2,1)} %bitcast.9) | data formatting | bytes 884736 | tf_op jit(solution)/shard_map/transpose | solution.py:469
  19.2 0.0 copy-done.5
  19.2 0.0 copy-done
  19.2 0.0 copy-done.1
  19.2 0.0 copy-done.4
  19.3 11.6 %shard_map.103 = (bf16[4,12,48,96]{3,2,1,0:T(8,128)(2,1)S(1)}, bf16[8,48,384]{2,1,0:T(8,128)(2,1)S(1)}, bf16[2,16,1664]{2,1,0:T(8,128)(2,1)S(1)}) custom-call(s32[1]{0:T(128)S(6)} %copy.17.shift_ref, bf16[48,12,384]{2,1,0:T(8,128)(2,1)S(1)} %bitcast.20, bf16[48,12,384]{2,1,0:T(8,128)(2,1)S(1)} %bitcast.21, bf16[2,48,6,384]{3,2,1,0:T(8,128)(2,1)S(1)} %bitcast.18, ...), custom_call_target="tpu_custom_call" | custom-call | flops 1000000000 | bytes 10000000 | tf_op jit(solution)/shard_map/pallas_call | solution.py:232
  30.8 19.7 %shard_map.104 = (bf16[12,48,96]{2,1,0:T(8,128)(2,1)S(1)}, bf16[12,48,96]{2,1,0:T(8,128)(2,1)S(1)}, bf16[8,48,384]{2,1,0:T(8,128)(2,1)S(1)}, bf16[8,16,1664]{2,1,0:T(8,128)(2,1)S(1)}, s32[4,16,128]{2,1,0:T(8,128)S(1)}) custom-call(s32[1]{0:T(128)S(6)} %copy.17.shift_ref, bf16[4,12,48,96]{3,2,1,0:T(8,128)(2,1)S(1)} %get-tuple-element.21.piece_ref, ...), custom_call_target="tpu_custom_call" | custom-call | tf_op jit(solution)/shard_map/pallas_call | solution.py:377
  50.6 2.2 %shard_map.105 = (bf16[6,12,8,96]{3,2,1,0:T(8,128)(2,1)}, f32[3,96,384]{2,1,0:T(8,128)}, f32[96,384]{1,0:T(8,128)}, f32[3,64,3312]{2,1,0:T(8,128)}) custom-call(s32[1]{0:T(128)S(6)} %copy.17.shift_ref, bf16[12,48,96]{2,1,0:T(8,128)(2,1)S(1)} %get-tuple-element.25.own_ref, bf16[12,48,96]{2,1,0:T(8,128)(2,1)S(1)} %get-tuple-element.26.edge_ref, ...), custom_call_target="tpu_custom_call" | custom-call | tf_op jit(solution)/shard_map/pallas_call | solution.py:445
Async XLA Ops:
  0.6 6.1 %copy-start.7 = (bf16[8,6,12,384]{3,0,2,1:T(8,128)(2,1)S(1)}, bf16[8,6,12,384]{3,0,2,1:T(8,128)(2,1)}, u32[]{:S(2)}) copy-start(bf16[8,6,12,384]{3,0,2,1:T(8,128)(2,1)} %param.7) | copy-start | bytes 1327108
  0.6 7.0 %copy-start.8 = (bf16[8,6,12,384]{3,0,2,1:T(8,128)(2,1)S(1)}, bf16[8,6,12,384]{3,0,2,1:T(8,128)(2,1)}, u32[]{:S(2)}) copy-start(bf16[8,6,12,384]{3,0,2,1:T(8,128)(2,1)} %param.13) | copy-start | bytes 1327108
  1.4 7.2 %copy-start.6 = (f32[64,3,3312]{2,0,1:T(8,128)S(1)}, f32[64,3,3312]{2,0,1:T(8,128)}, u32[]{:S(2)}) copy-start(f32[64,3,3312]{2,0,1:T(8,128)} %param.10) | copy-start | bytes 7630852
  3.7 14.4 %collective-permute-start = (bf16[2,6,6,8,384]{4,3,2,1,0:T(8,128)(2,1)}, bf16[2,6,6,8,384]{4,3,2,1,0:T(8,128)(2,1)}, u32[]{:S(2)}, u32[]{:S(2)}) collective-permute-start(bf16[2,6,6,8,384]{4,3,2,1,0:T(8,128)(2,1)} %maximum_select_fusion), channel_id=1, source_target_pairs={{0,16},{16,0},{1,17},{17,1},{2,18},{18,2},{3,19},{19,3},{4,20},{20... | collective-permute-start | bytes 1327112 | tf_op jit(solution)/shard_map/ppermute | solution.py:24
  8.5 1.8 %copy-start.9 = (s32[4,1]{0,1:T(1,128)S(1)}, s32[4,1]{0,1:T(1,128)}, u32[]{:S(2)}) copy-start(s32[4,1]{0,1:T(1,128)} %param.11) | copy-start | bytes 52
  10.3 8.9 %copy-start.5 = (bf16[96,384]{1,0:T(8,128)(2,1)S(1)}, bf16[96,384]{1,0:T(8,128)(2,1)}, u32[]{:S(2)}) copy-start(bf16[96,384]{1,0:T(8,128)(2,1)} %ow_ref.1) | copy-start | bytes 221188
  12.2 7.0 %copy-start = (bf16[8,6,12,384]{3,2,1,0:T(8,128)(2,1)S(1)}, bf16[8,6,12,384]{3,2,1,0:T(8,128)(2,1)}, u32[]{:S(2)}) copy-start(bf16[8,6,12,384]{3,2,1,0:T(8,128)(2,1)} %copy.11) | copy-start | bytes 1327108
  12.2 7.0 %copy-start.1 = (bf16[8,6,12,384]{3,2,1,0:T(8,128)(2,1)S(1)}, bf16[8,6,12,384]{3,2,1,0:T(8,128)(2,1)}, u32[]{:S(2)}) copy-start(bf16[8,6,12,384]{3,2,1,0:T(8,128)(2,1)} %copy.12) | copy-start | bytes 1327108
  12.2 7.0 %copy-start.4 = (bf16[3,384,96]{2,1,0:T(8,128)(2,1)S(1)}, bf16[3,384,96]{2,1,0:T(8,128)(2,1)}, u32[]{:S(2)}) copy-start(bf16[3,384,96]{2,1,0:T(8,128)(2,1)} %copy.16.aw_ref) | copy-start | bytes 663556
  15.8 1.1 %copy-start.2 = (f32[3072,128]{1,0:T(8,128)}, f32[3072,128]{1,0:T(8,128)S(1)}, u32[]{:S(2)}) copy-start(f32[3072,128]{1,0:T(8,128)S(1)} %get-tuple-element.19.from_a) | copy-start | bytes 4718596
  16.9 1.2 %copy-start.3 = (f32[3072,128]{1,0:T(8,128)}, f32[3072,128]{1,0:T(8,128)S(1)}, u32[]{:S(2)}) copy-start(f32[3072,128]{1,0:T(8,128)S(1)} %get-tuple-element.20.from_b) | copy-start | bytes 4718596
